TPU v7x, 256 devices: a whole 4x4x8 slice. The times are simulated.
256 devices in a mesh: seq: 16 (over z, core), heads: 4 (over x), batch: 4 (over y).
Axes of the slice: x: 4, y: 4, z: 8, core: 2. Of those that a mesh axis runs over, the one named last changes fastest.
Arguments:
- queries: bfloat16 [4, 4096, 8192], P('batch', 'seq', 'heads'), may hold values from -160 to 160
- keys: bfloat16 [4, 4096, 1024], P('batch', 'seq', 'heads'), may hold values from -7 to 7
- values: bfloat16 [4, 4096, 1024], P('batch', 'seq', 'heads'), may hold values from -6 to 6
- doc_lengths: int32 [4, 16], P('batch'), may hold values from 1 to 2176, 4096 in all within a row
- out_weight: bfloat16 [8192, 8192], P('heads', 'batch'), may hold values from -0.0625 to 0.0625
Outputs:
- projected: bfloat16 [4, 4096, 8192], P('heads', 'seq', 'batch')
Inputs may be any that keep to these rules, and one draw needn't show every extreme that they name: `doc_lengths`: each row sums to 4096; no document is longer than 2176 tokens and one is exactly 2176.
All inputs are finite; a program needn't handle non-finite values.
Results may differ from a plain program's by a relative error of at most 0.012.
Values may be sent and summed in bfloat16 or wider, within the bound.
A program may use at most 64 MiB of HBM per device.

v0:
```python
import jax
import jax.numpy as jnp
from jax import lax
from jax.sharding import PartitionSpec as P

HEAD_WIDTH = 128
DOCS = 16


def shifted(x, axis, by):
    peers = lax.axis_size(axis)
    pairs = [(i, i + by) for i in range(peers) if 0 <= i + by < peers]
    return lax.ppermute(x, axis, pairs)


def per_device(queries, keys, values, doc_lengths, out_weight):
    shard_len = queries.shape[1]
    q_width = queries.shape[2]
    kv_width = keys.shape[2]
    kv_heads = kv_width // HEAD_WIDTH
    q_groups = q_width // kv_width
    seq_total = lax.axis_size("seq") * shard_len
    shard_start = lax.axis_index("seq") * shard_len
    doc_ends = jnp.cumsum(doc_lengths[0])
    doc_starts = doc_ends - doc_lengths[0]
    all_positions = jnp.arange(seq_total, dtype=jnp.int32)
    doc_of = jnp.sum((all_positions[:, None] >= doc_ends[None, :]).astype(jnp.int32), axis=1)
    query_pos = shard_start + jnp.arange(shard_len, dtype=jnp.int32)
    query_doc = lax.dynamic_slice_in_dim(doc_of, shard_start, shard_len, 0)
    reach_start = jnp.sum(
        jnp.where(jnp.arange(DOCS, dtype=jnp.int32) == query_doc[0], doc_starts, 0)
    )
    query_heads = queries[0].reshape(shard_len, kv_heads, q_groups, HEAD_WIDTH)
    factor = HEAD_WIDTH ** (-0.5)

    def absorb(carried, key_block, value_block, key_start):
        key_count = key_block.shape[0]

        def attend(current):
            running, totals, weighted = current
            key_heads = key_block.reshape(key_count, kv_heads, HEAD_WIDTH)
            value_heads = value_block.reshape(key_count, kv_heads, HEAD_WIDTH)
            scores = (
                jnp.einsum(
                    "qhgd,khd->hgqk", query_heads, key_heads, preferred_element_type=jnp.float32
                )
                * factor
            )
            key_pos = key_start + jnp.arange(key_count, dtype=jnp.int32)
            key_doc = lax.dynamic_slice_in_dim(doc_of, key_start, key_count, 0)
            allowed = (query_doc[:, None] == key_doc[None, :]) & (
                key_pos[None, :] <= query_pos[:, None]
            )
            scores = jnp.where(allowed, scores, -jnp.inf)
            raised = jnp.maximum(running, jnp.max(scores, axis=-1))
            shrink = jnp.exp(running - raised)
            weights = jnp.exp(scores - raised[..., None])
            totals = totals * shrink + jnp.sum(weights, axis=-1)
            summed = jnp.einsum(
                "hgqk,khd->qhgd",
                weights.astype(jnp.bfloat16),
                value_heads,
                preferred_element_type=jnp.float32,
            )
            weighted = weighted * jnp.transpose(shrink, (2, 0, 1))[..., None] + summed
            return (raised, totals, weighted)

        needed = (
            (key_start >= 0)
            & (key_start + key_count > reach_start)
            & (key_start < shard_start + shard_len)
        )
        return lax.cond(needed, attend, lambda current: current, carried)

    initial = (
        jnp.full((kv_heads, q_groups, shard_len), -1e30, jnp.float32),
        jnp.zeros((kv_heads, q_groups, shard_len), jnp.float32),
        jnp.zeros((shard_len, kv_heads, q_groups, HEAD_WIDTH), jnp.float32),
    )
    longest = seq_total // 2 + shard_len // 2
    reach_back = min((longest + shard_len - 2) // shard_len, lax.axis_size("seq") - 1)
    finished = absorb(initial, keys[0], values[0], shard_start)
    stacked = jnp.stack((keys[0], values[0]))
    for distance in range(1, reach_back + 1):
        earlier = shifted(stacked, "seq", distance)
        finished = absorb(finished, earlier[0], earlier[1], shard_start - distance * shard_len)
    running, totals, weighted = finished
    attended = (weighted / jnp.transpose(totals, (2, 0, 1))[..., None]).astype(jnp.bfloat16)
    attended = attended.reshape(1, shard_len, q_width)
    gathered = lax.all_gather(attended, "batch", axis=0, tiled=True)
    flat_rows = gathered.reshape(-1, q_width)
    owned_rows = lax.psum_scatter(
        jnp.dot(flat_rows, out_weight, preferred_element_type=jnp.float32).astype(jnp.bfloat16),
        "heads",
        scatter_dimension=0,
        tiled=True,
    )
    return owned_rows.reshape(-1, shard_len, out_weight.shape[1])


def solution(mesh):
    return jax.shard_map(
        per_device,
        mesh=mesh,
        in_specs=(
            P("batch", "seq", "heads"),
            P("batch", "seq", "heads"),
            P("batch", "seq", "heads"),
            P("batch", None),
            P("heads", "batch"),
        ),
        out_specs=P("heads", "seq", "batch"),
        check_vma=False,
    )
```

profile of v0, /device:TPU:1, one launch (start us, length us, event | category | flops | bytes accessed | tf_op | source)
XLA Modules:
  0.0 296.8 jit_solution(16229299459573163268)
XLA Ops:
  9.3 4.9 %collective-permute-start = (bf16[2,256,256]{1,2,0:T(8,128)(2,1)}, bf16[2,256,256]{1,2,0:T(8,128)(2,1)}, u32[]{:S(2)}, u32[]{:S(2)}) collective-permute-start(bf16[2,256,256]{1,2,0:T(8,128)(2,1)} %pad_maximum_fusion), channel_id=1, source_target_pairs={{0,16},{16,32},{32,48},{48,64},{64,80},{80,96},{96,112},{112,128},... | collective-permute-start | bytes 786440 | tf_op jit(solution)/shard_map/ppermute | solution.py:13
  14.2 4.3 %collective-permute-start.1 = (bf16[2,256,256]{1,2,0:T(8,128)(2,1)}, bf16[2,256,256]{1,2,0:T(8,128)(2,1)}, u32[]{:S(2)}, u32[]{:S(2)}) collective-permute-start(bf16[2,256,256]{1,2,0:T(8,128)(2,1)} %pad_maximum_fusion), channel_id=1, source_target_pairs={{0,32},{16,48},{32,64},{48,80},{64,96},{80,112},{96,128},{112,144}... | collective-permute-start | bytes 786440 | tf_op jit(solution)/shard_map/ppermute | solution.py:13
  18.5 3.5 %collective-permute-start.2 = (bf16[2,256,256]{1,2,0:T(8,128)(2,1)}, bf16[2,256,256]{1,2,0:T(8,128)(2,1)}, u32[]{:S(2)}, u32[]{:S(2)}) collective-permute-start(bf16[2,256,256]{1,2,0:T(8,128)(2,1)} %pad_maximum_fusion), channel_id=1, source_target_pairs={{0,48},{16,64},{32,80},{48,96},{64,112},{80,128},{96,144},{112,160... | collective-permute-start | bytes 786440 | tf_op jit(solution)/shard_map/ppermute | solution.py:13
  22.0 5.2 %collective-permute-start.3 = (bf16[2,256,256]{1,2,0:T(8,128)(2,1)}, bf16[2,256,256]{1,2,0:T(8,128)(2,1)}, u32[]{:S(2)}, u32[]{:S(2)}) collective-permute-start(bf16[2,256,256]{1,2,0:T(8,128)(2,1)} %pad_maximum_fusion), channel_id=1, source_target_pairs={{0,64},{16,80},{32,96},{48,112},{64,128},{80,144},{96,160},{112,17... | collective-permute-start | bytes 786440 | tf_op jit(solution)/shard_map/ppermute | solution.py:13
  27.2 3.4 %collective-permute-start.4 = (bf16[2,256,256]{1,2,0:T(8,128)(2,1)}, bf16[2,256,256]{1,2,0:T(8,128)(2,1)}, u32[]{:S(2)}, u32[]{:S(2)}) collective-permute-start(bf16[2,256,256]{1,2,0:T(8,128)(2,1)} %pad_maximum_fusion), channel_id=1, source_target_pairs={{0,80},{16,96},{32,112},{48,128},{64,144},{80,160},{96,176},{112,1... | collective-permute-start | bytes 786440 | tf_op jit(solution)/shard_map/ppermute | solution.py:13
  32.2 1.3 dynamic_slice.33
  34.7 2.0 fusion.144
  44.1 1.5 copy.243
  45.6 10.9 %conditional.10 = (f32[2,8,256]{2,1,0:T(8,128)}, f32[2,8,256]{2,1,0:T(8,128)S(1)}, f32[256,2,8,128]{3,0,2,1:T(8,128)S(1)}) conditional(s32[]{:T(128)} %convert_element_type.79, () %tuple.68, (s32[256]{0:T(256)}, s32[]{:T(128)}, s32[4096]{0:T(1024)}, s32[256]{0:T(256)}, bf16[1,256,256]{2,1,0:T(8,128)(2,1)}, ...), branch_computations={%region_3.4_spmd, %region_4.7_spmd} | conditional | flops 549142784 | bytes 34266232 | solution.py:73
  49.6 1.3 copy-done
  50.9 1.6 fusion.1
  53.2 3.3 %bitcast_add_fusion = f32[256,2,8,128]{3,0,2,1:T(8,128)S(1)} fusion(f32[2,256,256,8]{2,1,3,0:T(8,128)} %copy-done, f32[2,8,256]{2,1,0:T(8,128)} %get-tuple-element.850, pred[256,256]{0,1:T(8,128)(4,1)S(1)} %compare_and_fusion, f32[256,2,8]{0,2,1:T(8,128)S(1)} %get-tuple-element.789, bf16[256,2,128,1]{2,1,0,3:T(2,128)(2,1)S(1)} %bitcast.314), kind=kOutput, calls=%fused_computation.6 | convolution fusion | flops 273154048 | bytes 6520832 | tf_op jit(solution)/shard_map/cond/branch_1_fun/hgqk,khd->qhgd/dot_general | solution.py:59
  56.5 1.3 collective-permute-start.5
  57.9 1.7 fusion.153
  59.5 2.3 collective-permute-start.6
  61.8 1.7 fusion.152
  63.5 2.0 collective-permute-start.7
  65.5 1.7 fusion.151
  67.1 2.0 collective-permute-start.8
  69.1 1.6 fusion.150
  70.8 1.6 fusion.149
  73.0 8.6 %conditional.11 = ((f32[2,8,256]{2,1,0:T(8,128)}, f32[2,8,256]{2,1,0:T(8,128)S(1)}, f32[256,2,8,128]{3,0,2,1:T(8,128)S(1)})) conditional(s32[]{:T(128)} %convert_element_type.78, (f32[2,8,256]{2,1,0:T(8,128)}, f32[2,8,256]{2,1,0:T(8,128)S(1)}, f32[256,2,8,128]{3,0,2,1:T(8,128)S(1)}) %conditional.10, (s32[256]{0:T(256)}, s32[]{:T(128)}, ...), branch_computations={%region_7.8_spmd, %region_8.11_spmd} | conditional | flops 549662976 | bytes 19143782 | solution.py:73
  75.2 1.7 fusion.20
  79.9 1.7 bitcast_add_fusion.1
  84.1 8.2 %collective-permute-done.8 = bf16[2,256,256]{1,2,0:T(8,128)(2,1)} collective-permute-done((bf16[2,256,256]{1,2,0:T(8,128)(2,1)}, bf16[2,256,256]{1,2,0:T(8,128)(2,1)}, u32[]{:S(2)}, u32[]{:S(2)}) %collective-permute-start.8) | collective-permute-done | bytes 262176 | tf_op jit(solution)/shard_map/ppermute | solution.py:13
  92.2 1.8 conditional.19
  92.2 1.8 copy.380
  94.1 1.8 divide_convert_fusion
  95.9 1.4 copy.271
  97.6 128.6 %all-gather.2.cloned.1.call-done = bf16[4,256,2048]{2,1,0:T(8,128)(2,1)} async-done(((bf16[1,256,2048]{2,1,0:T(8,128)(2,1)}), bf16[4,256,2048]{2,1,0:T(8,128)(2,1)}) %all-gather.2.cloned.1.call-update) | async-done | bytes 4194320 | tf_op jit(solution)/shard_map/all_gather | solution.py:90
  226.2 13.8 %convolution_convert_fusion = bf16[1024,2048]{1,0:T(8,128)(2,1)} fusion(bf16[1024,2048]{1,0:T(8,128)(2,1)} %bitcast.316, bf16[2048,2048]{1,0:T(8,128)(2,1)} %param.29), kind=kOutput, calls=%fused_computation.184 | convolution fusion | flops 8592031744 | bytes 16777216 | tf_op jit(solution)/shard_map/dot_general | solution.py:93
  240.0 50.0 %reduce-scatter.2.cloned.1.call-done = bf16[256,2048]{1,0:T(8,128)(2,1)} async-done(((bf16[1024,2048]{1,0:T(8,128)(2,1)}), bf16[256,2048]{1,0:T(8,128)(2,1)}) %reduce-scatter.2.cloned.1.call-update) | async-done | bytes 1048592 | tf_op jit(solution)/shard_map/reduce_scatter | solution.py:92
  (52 shorter events, 19.2 us)
Async XLA Ops:
  6.5 219.7 %all-gather.2.cloned.1.call-start = ((), (), s32[]{:S(2)}) async-start(), calls=%async_computation.1 | async-start | bytes 5242880 | tf_op jit(solution)/shard_map/all_gather | solution.py:90
  9.3 47.2 %collective-permute-start = (bf16[2,256,256]{1,2,0:T(8,128)(2,1)}, bf16[2,256,256]{1,2,0:T(8,128)(2,1)}, u32[]{:S(2)}, u32[]{:S(2)}) collective-permute-start(bf16[2,256,256]{1,2,0:T(8,128)(2,1)} %pad_maximum_fusion), channel_id=1, source_target_pairs={{0,16},{16,32},{32,48},{48,64},{64,80},{80,96},{96,112},{112,128},... | collective-permute-start | bytes 786440 | tf_op jit(solution)/shard_map/ppermute | solution.py:13
  14.2 45.3 %collective-permute-start.1 = (bf16[2,256,256]{1,2,0:T(8,128)(2,1)}, bf16[2,256,256]{1,2,0:T(8,128)(2,1)}, u32[]{:S(2)}, u32[]{:S(2)}) collective-permute-start(bf16[2,256,256]{1,2,0:T(8,128)(2,1)} %pad_maximum_fusion), channel_id=1, source_target_pairs={{0,32},{16,48},{32,64},{48,80},{64,96},{80,112},{96,128},{112,144}... | collective-permute-start | bytes 786440 | tf_op jit(solution)/shard_map/ppermute | solution.py:13
  18.5 45.0 %collective-permute-start.2 = (bf16[2,256,256]{1,2,0:T(8,128)(2,1)}, bf16[2,256,256]{1,2,0:T(8,128)(2,1)}, u32[]{:S(2)}, u32[]{:S(2)}) collective-permute-start(bf16[2,256,256]{1,2,0:T(8,128)(2,1)} %pad_maximum_fusion), channel_id=1, source_target_pairs={{0,48},{16,64},{32,80},{48,96},{64,112},{80,128},{96,144},{112,160... | collective-permute-start | bytes 786440 | tf_op jit(solution)/shard_map/ppermute | solution.py:13
  22.0 45.1 %collective-permute-start.3 = (bf16[2,256,256]{1,2,0:T(8,128)(2,1)}, bf16[2,256,256]{1,2,0:T(8,128)(2,1)}, u32[]{:S(2)}, u32[]{:S(2)}) collective-permute-start(bf16[2,256,256]{1,2,0:T(8,128)(2,1)} %pad_maximum_fusion), channel_id=1, source_target_pairs={{0,64},{16,80},{32,96},{48,112},{64,128},{80,144},{96,160},{112,17... | collective-permute-start | bytes 786440 | tf_op jit(solution)/shard_map/ppermute | solution.py:13
  27.2 43.5 %collective-permute-start.4 = (bf16[2,256,256]{1,2,0:T(8,128)(2,1)}, bf16[2,256,256]{1,2,0:T(8,128)(2,1)}, u32[]{:S(2)}, u32[]{:S(2)}) collective-permute-start(bf16[2,256,256]{1,2,0:T(8,128)(2,1)} %pad_maximum_fusion), channel_id=1, source_target_pairs={{0,80},{16,96},{32,112},{48,128},{64,144},{80,160},{96,176},{112,1... | collective-permute-start | bytes 786440 | tf_op jit(solution)/shard_map/ppermute | solution.py:13
  48.2 5.0 %copy-start.4 = (bf16[1,256,256]{2,1,0:T(8,128)(2,1)S(1)}, bf16[1,256,256]{2,1,0:T(8,128)(2,1)}, u32[]{:S(2)}) copy-start(bf16[1,256,256]{2,1,0:T(8,128)(2,1)} %get-tuple-element.259) | copy-start | bytes 393220 | tf_op jit(solution)/shard_map/cond
  49.0 1.9 copy-start
  56.5 15.9 %collective-permute-start.5 = (bf16[2,256,256]{1,2,0:T(8,128)(2,1)}, bf16[2,256,256]{1,2,0:T(8,128)(2,1)S(1)}, u32[]{:S(2)}, u32[]{:S(2)}) collective-permute-start(bf16[2,256,256]{1,2,0:T(8,128)(2,1)} %pad_maximum_fusion), channel_id=1, source_target_pairs={{0,96},{16,112},{32,128},{48,144},{64,160},{80,176},{96,192},{112,... | collective-permute-start | bytes 786440 | tf_op jit(solution)/shard_map/ppermute | solution.py:13
  59.5 23.3 %collective-permute-start.6 = (bf16[2,256,256]{1,2,0:T(8,128)(2,1)}, bf16[2,256,256]{1,2,0:T(8,128)(2,1)}, u32[]{:S(2)}, u32[]{:S(2)}) collective-permute-start(bf16[2,256,256]{1,2,0:T(8,128)(2,1)} %pad_maximum_fusion), channel_id=1, source_target_pairs={{0,112},{16,128},{32,144},{48,160},{64,176},{80,192},{96,208},{112... | collective-permute-start | bytes 786440 | tf_op jit(solution)/shard_map/ppermute | solution.py:13
  63.5 20.5 %collective-permute-start.7 = (bf16[2,256,256]{1,2,0:T(8,128)(2,1)}, bf16[2,256,256]{1,2,0:T(8,128)(2,1)}, u32[]{:S(2)}, u32[]{:S(2)}) collective-permute-start(bf16[2,256,256]{1,2,0:T(8,128)(2,1)} %pad_maximum_fusion), channel_id=1, source_target_pairs={{0,128},{16,144},{32,160},{48,176},{64,192},{80,208},{96,224},{112... | collective-permute-start | bytes 786440 | tf_op jit(solution)/shard_map/ppermute | solution.py:13
  67.1 25.1 %collective-permute-start.8 = (bf16[2,256,256]{1,2,0:T(8,128)(2,1)}, bf16[2,256,256]{1,2,0:T(8,128)(2,1)}, u32[]{:S(2)}, u32[]{:S(2)}) collective-permute-start(bf16[2,256,256]{1,2,0:T(8,128)(2,1)} %pad_maximum_fusion), channel_id=1, source_target_pairs={{0,144},{16,160},{32,176},{48,192},{64,208},{80,224},{96,240},{1,1... | collective-permute-start | bytes 786440 | tf_op jit(solution)/shard_map/ppermute | solution.py:13
  75.2 4.7 %copy-start.3 = (bf16[1,256,256]{1,2,0:T(8,128)(2,1)S(1)}, bf16[1,256,256]{1,2,0:T(8,128)(2,1)}, u32[]{:S(2)}) copy-start(bf16[1,256,256]{1,2,0:T(8,128)(2,1)} %get-tuple-element.707) | copy-start | bytes 393220 | tf_op jit(solution)/shard_map/cond
  81.9 0.9 copy-start.5
  97.3 192.7 %reduce-scatter.2.cloned.1.call-start = ((), (), s32[]{:S(2)}) async-start(), calls=%async_computation.2 | async-start | bytes 5242880 | tf_op jit(solution)/shard_map/reduce_scatter | solution.py:92
Sparse Core Ops, SparseCore 0:
  97.4 128.7 all-gather.1
  240.2 49.7 reduce-scatter.1
where the time goes:
time: 300 us; the launch traced here: 297 us
  waiting for transfers between devices  187 us (62%)
  starting transfers between devices  29.2 us (10%)
  local copies, waits for them, and re-layouts  25.2 us (8%)
  matrix products  21.3 us (7%)
  between operations  20.4 us (7%)
  other arithmetic  13.4 us (4%)
    all_gather x1, waiting for transfers between devices, per_device(): gathered = lax.all_gather(attended, 'batch', axis=0, tiled=True)  129 us
    reduce_scatter x1, waiting for transfers between devices, per_device(): lax.psum_scatter(jnp.dot(flat_rows, out_weight, preferred_element_type=jn...  50 us
    ppermute x9, starting transfers between devices, shifted(): return lax.ppermute(x, axis, pairs)  28.9 us
    dot_general x1, matrix products, per_device(): jnp.dot(flat_rows, out_weight, preferred_element_type=jnp.float32)  13.8 us
    slice x7, local copies, waits for them, and re-layouts, per_device(): earlier[1]  9.95 us
    ppermute x9, waiting for transfers between devices, shifted(): return lax.ppermute(x, axis, pairs)  8.21 us
  transfers between devices with their start and end apart: 11, of which 3 were waited for; matrix products, arithmetic and copies ran while one was open for 12% of the time, Pallas kernels for 0%

commit v1 on v0

--- a/solution.py
+++ b/solution.py
@@ -87,7 +87,11 @@
     running, totals, weighted = finished
     attended = (weighted / jnp.transpose(totals, (2, 0, 1))[..., None]).astype(jnp.bfloat16)
     attended = attended.reshape(1, shard_len, q_width)
-    gathered = lax.all_gather(attended, "batch", axis=0, tiled=True)
+    length = lax.axis_size("batch")
+    repeats = [length if d == 0 else 1 for d in range(attended.ndim)]
+    gathered = lax.all_to_all(
+        jnp.tile(attended, repeats), "batch", split_axis=0, concat_axis=0, tiled=True
+    )
     flat_rows = gathered.reshape(-1, q_width)
     owned_rows = lax.psum_scatter(
         jnp.dot(flat_rows, out_weight, preferred_element_type=jnp.float32).astype(jnp.bfloat16),

time: 300 us -> 290 us (0.967)
  waiting for transfers between devices: 187 us -> 139 us
  blocking collectives: 0 us -> 40.3 us
    all_gather x1 -> x0, waiting for transfers between devices: 129 us -> none  [per_device(): gathered = lax.all_gather(attended, 'batch', axis=0, tiled=True)]
    reduce_scatter x1, waiting for transfers between devices: 50 us -> 130 us  [per_device(): lax.psum_scatter(jnp.dot(flat_rows, out_weight, preferred_element_type=jn...]
    all_to_all x0 -> x1, blocking collectives: none -> 40.3 us  [per_device(): lax.all_to_all(jnp.tile(attended, repeats), 'batch', split_axis=0, concat...]
  transfers between devices with their start and end apart: 11 -> 10, of which waited for: 3 -> 2; matrix products, arithmetic and copies ran while one was open for 12% -> 13% of each run, Pallas kernels for 0% -> 0%
where the time goes in v1:
time: 290 us; the launch traced here: 287 us
  waiting for transfers between devices  139 us (48%)
  blocking collectives  40.3 us (14%)
  starting transfers between devices  28.9 us (10%)
  local copies, waits for them, and re-layouts  24.1 us (8%)
  between operations  20.4 us (7%)
  matrix products  20 us (7%)
  other arithmetic  13.4 us (5%)
    reduce_scatter x1, waiting for transfers between devices, per_device(): lax.psum_scatter(jnp.dot(flat_rows, out_weight, preferred_element_type=jn...  130 us
    all_to_all x1, blocking collectives, per_device(): lax.all_to_all(jnp.tile(attended, repeats), 'batch', split_axis=0, concat...  40.3 us
    ppermute x9, starting transfers between devices, shifted(): return lax.ppermute(x, axis, pairs)  28.9 us
    dot_general x1, matrix products, per_device(): jnp.dot(flat_rows, out_weight, preferred_element_type=jnp.float32)  12.6 us
    slice x7, local copies, waits for them, and re-layouts, per_device(): earlier[1]  9.95 us
    ppermute x9, waiting for transfers between devices, shifted(): return lax.ppermute(x, axis, pairs)  9.07 us
  transfers between devices with their start and end apart: 10, of which 2 were waited for; matrix products, arithmetic and copies ran while one was open for 13% of the time, Pallas kernels for 0%

profile of v1, /device:TPU:1, one launch (start us, length us, event | category | flops | bytes accessed | tf_op | source)
XLA Modules:
  0.0 286.5 jit_solution(9016196186086732165)
XLA Ops:
  9.3 4.9 %collective-permute-start = (bf16[2,256,256]{1,2,0:T(8,128)(2,1)}, bf16[2,256,256]{1,2,0:T(8,128)(2,1)}, u32[]{:S(2)}, u32[]{:S(2)}) collective-permute-start(bf16[2,256,256]{1,2,0:T(8,128)(2,1)} %pad_maximum_fusion), channel_id=1, source_target_pairs={{0,16},{16,32},{32,48},{48,64},{64,80},{80,96},{96,112},{112,128},... | collective-permute-start | bytes 786440 | tf_op jit(solution)/shard_map/ppermute | solution.py:13
  14.2 4.3 %collective-permute-start.1 = (bf16[2,256,256]{1,2,0:T(8,128)(2,1)}, bf16[2,256,256]{1,2,0:T(8,128)(2,1)}, u32[]{:S(2)}, u32[]{:S(2)}) collective-permute-start(bf16[2,256,256]{1,2,0:T(8,128)(2,1)} %pad_maximum_fusion), channel_id=1, source_target_pairs={{0,32},{16,48},{32,64},{48,80},{64,96},{80,112},{96,128},{112,144}... | collective-permute-start | bytes 786440 | tf_op jit(solution)/shard_map/ppermute | solution.py:13
  18.5 3.5 %collective-permute-start.2 = (bf16[2,256,256]{1,2,0:T(8,128)(2,1)}, bf16[2,256,256]{1,2,0:T(8,128)(2,1)}, u32[]{:S(2)}, u32[]{:S(2)}) collective-permute-start(bf16[2,256,256]{1,2,0:T(8,128)(2,1)} %pad_maximum_fusion), channel_id=1, source_target_pairs={{0,48},{16,64},{32,80},{48,96},{64,112},{80,128},{96,144},{112,160... | collective-permute-start | bytes 786440 | tf_op jit(solution)/shard_map/ppermute | solution.py:13
  22.0 5.2 %collective-permute-start.3 = (bf16[2,256,256]{1,2,0:T(8,128)(2,1)}, bf16[2,256,256]{1,2,0:T(8,128)(2,1)}, u32[]{:S(2)}, u32[]{:S(2)}) collective-permute-start(bf16[2,256,256]{1,2,0:T(8,128)(2,1)} %pad_maximum_fusion), channel_id=1, source_target_pairs={{0,64},{16,80},{32,96},{48,112},{64,128},{80,144},{96,160},{112,17... | collective-permute-start | bytes 786440 | tf_op jit(solution)/shard_map/ppermute | solution.py:13
  27.2 3.4 %collective-permute-start.4 = (bf16[2,256,256]{1,2,0:T(8,128)(2,1)}, bf16[2,256,256]{1,2,0:T(8,128)(2,1)}, u32[]{:S(2)}, u32[]{:S(2)}) collective-permute-start(bf16[2,256,256]{1,2,0:T(8,128)(2,1)} %pad_maximum_fusion), channel_id=1, source_target_pairs={{0,80},{16,96},{32,112},{48,128},{64,144},{80,160},{96,176},{112,1... | collective-permute-start | bytes 786440 | tf_op jit(solution)/shard_map/ppermute | solution.py:13
  32.2 1.3 dynamic_slice.33
  33.5 1.2 slice.61
  34.7 2.0 fusion.144
  44.1 1.5 copy.124
  45.6 10.9 %conditional.10 = (f32[2,8,256]{2,1,0:T(8,128)}, f32[2,8,256]{2,1,0:T(8,128)S(1)}, f32[256,2,8,128]{3,0,2,1:T(8,128)S(1)}) conditional(s32[]{:T(128)} %convert_element_type.79, () %tuple.68, (s32[256]{0:T(256)}, s32[]{:T(128)}, s32[4096]{0:T(1024)}, s32[256]{0:T(256)}, bf16[1,256,256]{2,1,0:T(8,128)(2,1)}, ...), branch_computations={%region_3.4_spmd, %region_4.7_spmd} | conditional | flops 549142784 | bytes 34266232 | solution.py:73
  49.6 1.3 copy-done
  50.9 1.6 fusion.1
  53.3 3.3 %bitcast_add_fusion = f32[256,2,8,128]{3,0,2,1:T(8,128)S(1)} fusion(f32[2,256,256,8]{2,1,3,0:T(8,128)} %copy-done, f32[2,8,256]{2,1,0:T(8,128)} %get-tuple-element.660, pred[256,256]{0,1:T(8,128)(4,1)S(1)} %compare_and_fusion, f32[256,2,8]{0,2,1:T(8,128)S(1)} %get-tuple-element.599, bf16[256,2,128,1]{2,1,0,3:T(2,128)(2,1)S(1)} %bitcast.315), kind=kOutput, calls=%fused_computation.6 | convolution fusion | flops 273154048 | bytes 6520832 | tf_op jit(solution)/shard_map/cond/branch_1_fun/hgqk,khd->qhgd/dot_general | solution.py:59
  56.5 1.3 collective-permute-start.5
  57.9 1.7 fusion.153
  59.5 2.3 collective-permute-start.6
  61.8 1.7 fusion.152
  63.5 2.0 collective-permute-start.7
  65.5 1.7 fusion.151
  67.1 2.0 collective-permute-start.8
  69.1 1.6 fusion.150
  70.8 1.6 fusion.149
  73.0 8.6 %conditional.11 = ((f32[2,8,256]{2,1,0:T(8,128)}, f32[2,8,256]{2,1,0:T(8,128)S(1)}, f32[256,2,8,128]{3,0,2,1:T(8,128)S(1)})) conditional(s32[]{:T(128)} %convert_element_type.78, (f32[2,8,256]{2,1,0:T(8,128)}, f32[2,8,256]{2,1,0:T(8,128)S(1)}, f32[256,2,8,128]{3,0,2,1:T(8,128)S(1)}) %conditional.10, (s32[256]{0:T(256)}, s32[]{:T(128)}, ...), branch_computations={%region_7.8_spmd, %region_8.11_spmd} | conditional | flops 549662976 | bytes 19143782 | solution.py:73
  75.2 1.7 fusion.20
  79.9 1.7 bitcast_add_fusion.1
  83.2 9.0 %collective-permute-done.8 = bf16[2,256,256]{1,2,0:T(8,128)(2,1)} collective-permute-done((bf16[2,256,256]{1,2,0:T(8,128)(2,1)}, bf16[2,256,256]{1,2,0:T(8,128)(2,1)}, u32[]{:S(2)}, u32[]{:S(2)}) %collective-permute-start.8) | collective-permute-done | bytes 262176 | tf_op jit(solution)/shard_map/ppermute | solution.py:13
  92.2 1.8 conditional.19
  92.2 1.8 copy.261
  94.1 1.8 divide_convert_fusion
  97.1 40.3 %all_to_all.5 = bf16[4,256,2048]{2,1,0:T(8,128)(2,1)S(1)} all-to-all(bf16[4,256,2048]{2,1,0:T(8,128)(2,1)S(1)} %tile.9), channel_id=1, replica_groups=mesh['seq'=16,'heads'=4,'batch'=4] {'batch'}, dimensions={0} | all-to-all | bytes 8388608 | tf_op jit(solution)/shard_map/all_to_all | solution.py:92
  137.5 12.6 %convolution_convert_fusion = bf16[1024,2048]{1,0:T(8,128)(2,1)} fusion(bf16[1024,2048]{1,0:T(8,128)(2,1)S(1)} %bitcast.294, bf16[2048,2048]{1,0:T(8,128)(2,1)} %param.29), kind=kOutput, calls=%fused_computation.184 | convolution fusion | flops 8592031744 | bytes 16777216 | tf_op jit(solution)/shard_map/dot_general | solution.py:97
  150.1 129.6 %reduce-scatter.2.cloned.1.call-done = bf16[256,2048]{1,0:T(8,128)(2,1)} async-done(((bf16[1024,2048]{1,0:T(8,128)(2,1)}), bf16[256,2048]{1,0:T(8,128)(2,1)}) %reduce-scatter.2.cloned.1.call-update) | async-done | bytes 1048592 | tf_op jit(solution)/shard_map/reduce_scatter | solution.py:96
  (49 shorter events, 18.1 us)
Async XLA Ops:
  6.5 273.1 %reduce-scatter.2.cloned.1.call-start = ((), (), s32[]{:S(2)}) async-start(), calls=%async_computation.2 | async-start | bytes 5242880 | tf_op jit(solution)/shard_map/reduce_scatter | solution.py:96
  9.3 47.2 %collective-permute-start = (bf16[2,256,256]{1,2,0:T(8,128)(2,1)}, bf16[2,256,256]{1,2,0:T(8,128)(2,1)}, u32[]{:S(2)}, u32[]{:S(2)}) collective-permute-start(bf16[2,256,256]{1,2,0:T(8,128)(2,1)} %pad_maximum_fusion), channel_id=1, source_target_pairs={{0,16},{16,32},{32,48},{48,64},{64,80},{80,96},{96,112},{112,128},... | collective-permute-start | bytes 786440 | tf_op jit(solution)/shard_map/ppermute | solution.py:13
  14.2 45.3 %collective-permute-start.1 = (bf16[2,256,256]{1,2,0:T(8,128)(2,1)}, bf16[2,256,256]{1,2,0:T(8,128)(2,1)}, u32[]{:S(2)}, u32[]{:S(2)}) collective-permute-start(bf16[2,256,256]{1,2,0:T(8,128)(2,1)} %pad_maximum_fusion), channel_id=1, source_target_pairs={{0,32},{16,48},{32,64},{48,80},{64,96},{80,112},{96,128},{112,144}... | collective-permute-start | bytes 786440 | tf_op jit(solution)/shard_map/ppermute | solution.py:13
  18.5 45.0 %collective-permute-start.2 = (bf16[2,256,256]{1,2,0:T(8,128)(2,1)}, bf16[2,256,256]{1,2,0:T(8,128)(2,1)}, u32[]{:S(2)}, u32[]{:S(2)}) collective-permute-start(bf16[2,256,256]{1,2,0:T(8,128)(2,1)} %pad_maximum_fusion), channel_id=1, source_target_pairs={{0,48},{16,64},{32,80},{48,96},{64,112},{80,128},{96,144},{112,160... | collective-permute-start | bytes 786440 | tf_op jit(solution)/shard_map/ppermute | solution.py:13
  22.0 45.1 %collective-permute-start.3 = (bf16[2,256,256]{1,2,0:T(8,128)(2,1)}, bf16[2,256,256]{1,2,0:T(8,128)(2,1)}, u32[]{:S(2)}, u32[]{:S(2)}) collective-permute-start(bf16[2,256,256]{1,2,0:T(8,128)(2,1)} %pad_maximum_fusion), channel_id=1, source_target_pairs={{0,64},{16,80},{32,96},{48,112},{64,128},{80,144},{96,160},{112,17... | collective-permute-start | bytes 786440 | tf_op jit(solution)/shard_map/ppermute | solution.py:13
  27.2 43.5 %collective-permute-start.4 = (bf16[2,256,256]{1,2,0:T(8,128)(2,1)}, bf16[2,256,256]{1,2,0:T(8,128)(2,1)}, u32[]{:S(2)}, u32[]{:S(2)}) collective-permute-start(bf16[2,256,256]{1,2,0:T(8,128)(2,1)} %pad_maximum_fusion), channel_id=1, source_target_pairs={{0,80},{16,96},{32,112},{48,128},{64,144},{80,160},{96,176},{112,1... | collective-permute-start | bytes 786440 | tf_op jit(solution)/shard_map/ppermute | solution.py:13
  48.2 5.0 %copy-start.4 = (bf16[1,256,256]{2,1,0:T(8,128)(2,1)S(1)}, bf16[1,256,256]{2,1,0:T(8,128)(2,1)}, u32[]{:S(2)}) copy-start(bf16[1,256,256]{2,1,0:T(8,128)(2,1)} %get-tuple-element.259) | copy-start | bytes 393220 | tf_op jit(solution)/shard_map/cond
  49.0 1.9 copy-start
  56.5 15.8 %collective-permute-start.5 = (bf16[2,256,256]{1,2,0:T(8,128)(2,1)}, bf16[2,256,256]{1,2,0:T(8,128)(2,1)S(1)}, u32[]{:S(2)}, u32[]{:S(2)}) collective-permute-start(bf16[2,256,256]{1,2,0:T(8,128)(2,1)} %pad_maximum_fusion), channel_id=1, source_target_pairs={{0,96},{16,112},{32,128},{48,144},{64,160},{80,176},{96,192},{112,... | collective-permute-start | bytes 786440 | tf_op jit(solution)/shard_map/ppermute | solution.py:13
  59.5 22.4 %collective-permute-start.6 = (bf16[2,256,256]{1,2,0:T(8,128)(2,1)}, bf16[2,256,256]{1,2,0:T(8,128)(2,1)}, u32[]{:S(2)}, u32[]{:S(2)}) collective-permute-start(bf16[2,256,256]{1,2,0:T(8,128)(2,1)} %pad_maximum_fusion), channel_id=1, source_target_pairs={{0,112},{16,128},{32,144},{48,160},{64,176},{80,192},{96,208},{112... | collective-permute-start | bytes 786440 | tf_op jit(solution)/shard_map/ppermute | solution.py:13
  63.5 19.7 %collective-permute-start.7 = (bf16[2,256,256]{1,2,0:T(8,128)(2,1)}, bf16[2,256,256]{1,2,0:T(8,128)(2,1)}, u32[]{:S(2)}, u32[]{:S(2)}) collective-permute-start(bf16[2,256,256]{1,2,0:T(8,128)(2,1)} %pad_maximum_fusion), channel_id=1, source_target_pairs={{0,128},{16,144},{32,160},{48,176},{64,192},{80,208},{96,224},{112... | collective-permute-start | bytes 786440 | tf_op jit(solution)/shard_map/ppermute | solution.py:13
  67.1 25.1 %collective-permute-start.8 = (bf16[2,256,256]{1,2,0:T(8,128)(2,1)}, bf16[2,256,256]{1,2,0:T(8,128)(2,1)}, u32[]{:S(2)}, u32[]{:S(2)}) collective-permute-start(bf16[2,256,256]{1,2,0:T(8,128)(2,1)} %pad_maximum_fusion), channel_id=1, source_target_pairs={{0,144},{16,160},{32,176},{48,192},{64,208},{80,224},{96,240},{1,1... | collective-permute-start | bytes 786440 | tf_op jit(solution)/shard_map/ppermute | solution.py:13
  75.2 4.7 %copy-start.3 = (bf16[1,256,256]{1,2,0:T(8,128)(2,1)S(1)}, bf16[1,256,256]{1,2,0:T(8,128)(2,1)}, u32[]{:S(2)}) copy-start(bf16[1,256,256]{1,2,0:T(8,128)(2,1)} %get-tuple-element.517) | copy-start | bytes 393220 | tf_op jit(solution)/shard_map/cond
Sparse Core Ops, SparseCore 0:
  150.2 129.4 reduce-scatter.1
